TPU v7x, 32 devices: a whole 2x2x4 slice. The times are simulated.
32 devices in a mesh: parts: 2 (over y), mem: 4 (over z), space: 4 (over x, core).
Axes of the slice: x: 2, y: 2, z: 4, core: 2. Of those that a mesh axis runs over, the one named last changes fastest.
Arguments:
- ensemble: bfloat16 [64, 70, 8192], P('mem', None, ('parts', 'space')), parts along dimension 2, may hold values from -6 to 6
- transform: bfloat16 [128, 64], P('parts'), parts along dimension 0, may hold values from -0.75 to 0.75
- obs_operator: bfloat16 [16, 70], replicated, may hold values from -0.75 to 0.75
- obs_weight: float32 [16, 8192], P(None, ('parts', 'space')), parts along dimension 1, may hold values from 0.25 to 40, as said below
Outputs:
- analysis: bfloat16 [64, 70, 8192], P('mem', None, ('parts', 'space')), parts along dimension 2
- prior_gram: float32 [128, 64], P('parts'), parts along dimension 0
- posterior_gram: float32 [128, 64], P('parts'), parts along dimension 0
There are 2 independent parts, one for each index of `parts`. A program takes and returns all parts, laid end to end along the dimension named above; an argument that names none is the same for every part. Nothing has to cross between parts.
Inputs may be any that keep to these rules, and one draw needn't show every extreme that they name: `obs_weight`: positive.
All inputs are finite; a program needn't handle non-finite values.
Results may differ from a plain program's by a relative error of at most 0.001.
Values may be sent and summed in bfloat16 or wider, within the bound.
A program may use at most 64 MiB of HBM per device.

v0:
```python
import jax
import jax.numpy as jnp
from jax import lax
from jax.sharding import PartitionSpec as P

MEMBERS = 64


HIGHEST = lax.Precision.HIGHEST


def gram_terms(observed, weights):
    departures = observed - jnp.sum(observed, axis=0) / MEMBERS
    weighted = departures * weights[None, :, :]
    partial_gram = jnp.einsum("ioc,joc->ij", weighted, departures, precision=HIGHEST)
    return (partial_gram, jnp.sum(weights))


def per_device(ensemble, transform, obs_operator, obs_weight):
    local_members = ensemble.shape[0]
    mixing = transform.astype(jnp.float32)
    own_start = lax.axis_index("mem") * local_members
    own_columns = lax.dynamic_slice_in_dim(transform, own_start, local_members, 1)
    keep_mean = 1.0 - jnp.sum(own_columns.astype(jnp.float32), axis=0)
    members_block = lax.all_gather(ensemble, "mem", axis=0, tiled=True)
    combined = jnp.einsum(
        "kj,kvc->jvc", own_columns, members_block, preferred_element_type=jnp.float32
    )
    totals = jnp.sum(members_block, axis=0, dtype=jnp.float32)
    results = (totals, combined)
    totals = results[0]
    combined = results[1]
    member_mean = totals / MEMBERS
    analysis = (combined + member_mean[None, :, :] * keep_mean[:, None, None]).astype(jnp.bfloat16)
    observed = jnp.einsum("ov,mvc->moc", obs_operator, ensemble, preferred_element_type=jnp.float32)
    by_columns = lax.all_to_all(
        observed.astype(jnp.bfloat16), "mem", split_axis=2, concat_axis=0, tiled=True
    ).astype(observed.dtype)
    cells_here = by_columns.shape[2]
    own_weights = lax.dynamic_slice_in_dim(
        obs_weight, lax.axis_index("mem") * cells_here, cells_here, 1
    )
    partial_gram, weight_sum = gram_terms(by_columns, own_weights)
    gram_sum, weight_total = lax.psum((partial_gram, weight_sum), ("mem", "space"))
    prior_gram = gram_sum / weight_total
    carried = jnp.dot(mixing.T, prior_gram, precision=HIGHEST)
    posterior_gram = jnp.dot(carried, mixing, precision=HIGHEST)
    return (analysis, prior_gram, posterior_gram)


def solution(mesh):
    return jax.shard_map(
        per_device,
        mesh=mesh,
        in_specs=(
            P("mem", None, ("parts", "space")),
            P("parts", None),
            P(),
            P(None, ("parts", "space")),
        ),
        out_specs=(P("mem", None, ("parts", "space")), P("parts", None), P("parts", None)),
        check_vma=False,
    )
```

profile of v0, /device:TPU:0, one launch (start us, length us, event | category | flops | bytes accessed | tf_op | source)
XLA Modules:
  0.0 202.9 jit_solution(353153275937876548)
XLA Ops:
  7.2 0.0 copy-start
  7.2 0.0 all-gather.2.cloned.1.call-start
  7.2 0.7 all-gather.2.cloned.1.call-update
  7.9 3.0 %fusion.7 = bf16[16,16,1024]{2,1,0:T(8,128)(2,1)S(1)} fusion(bf16[16,70,1024]{2,0,1:T(8,128)(2,1)} %param.4, bf16[16,70]{1,0:T(8,128)(2,1)} %param.6), kind=kOutput, calls=%fused_computation.8 | convolution fusion | flops 36962304 | bytes 2820288 | tf_op jit(solution)/shard_map/ov,mvc->moc/dot_general | solution.py:35
  10.9 4.7 %copy.25 = bf16[16,16,1024]{1,0,2:T(8,128)(2,1)} copy(bf16[16,16,1024]{2,1,0:T(8,128)(2,1)S(1)} %fusion.7) | data formatting | bytes 1048576 | tf_op jit(solution)/shard_map/convert_element_type | solution.py:37
  15.6 6.6 %reshape.27 = bf16[4,2,32768]{2,1,0:T(2,128)(2,1)} reshape(bf16[1024,16,16]{2,1,0:T(8,128)(2,1)} %bitcast.28) | data formatting | bytes 1048576
  22.2 6.4 %all-to-all-start = ((bf16[4,2,32768]{2,1,0:T(2,128)(2,1)}), bf16[4,2,32768]{2,1,0:T(2,128)(2,1)S(1)}, u32[]{:S(2)}, u32[]{:S(2)}) async-start(bf16[4,2,32768]{2,1,0:T(2,128)(2,1)} %reshape.27), calls=%async_computation | async-start | bytes 1048576 | tf_op jit(solution)/shard_map/all_to_all | solution.py:36
  28.6 0.0 copy-done
  28.6 0.1 constant_dynamic-slice_fusion.1
  28.7 0.1 copy.28
  28.8 0.1 convert_reduce_fusion.2
  28.9 1.3 fusion.16
  30.2 25.9 %all-to-all-done = bf16[4,2,32768]{2,1,0:T(2,128)(2,1)S(1)} async-done(((bf16[4,2,32768]{2,1,0:T(2,128)(2,1)}), bf16[4,2,32768]{2,1,0:T(2,128)(2,1)S(1)}, u32[]{:S(2)}, u32[]{:S(2)}) %all-to-all-start) | async-done | bytes 524320 | tf_op jit(solution)/shard_map/all_to_all | solution.py:36
  56.1 4.1 %reshape.28 = bf16[1024,16,16]{2,1,0:T(8,128)(2,1)} reshape(bf16[4,2,32768]{2,1,0:T(2,128)(2,1)S(1)} %all-to-all-done) | data formatting | bytes 1048576
  60.2 6.1 %bitcast_convert_fusion = f32[16,16,1024]{1,0,2:T(8,128)} fusion(bf16[1024,16,16]{2,1,0:T(8,128)(2,1)} %reshape.28), kind=kLoop, calls=%fused_computation.22 | loop fusion | flops 262144 | bytes 1572864 | tf_op jit(solution)/shard_map/convert_element_type | solution.py:38
  66.4 6.6 %copy.26 = f32[4,16,16,256]{3,1,0,2:T(8,128)S(1)} copy(f32[4,16,16,256]{2,1,3,0:T(8,128)} %bitcast.27) | data formatting | bytes 2097152 | tf_op jit(solution)/shard_map/convert_element_type | solution.py:38
  72.9 4.2 %convert_reduce_fusion.1 = f32[16,1024]{0,1:T(8,128)S(1)} fusion(bf16[1024,16,16]{2,1,0:T(8,128)(2,1)} %reshape.28), kind=kLoop, calls=%fused_computation.4 | loop fusion | flops 507904 | bytes 589824 | tf_op jit(solution)/shard_map/reduce_sum | solution.py:13
  77.2 0.1 copy.27
  77.3 0.1 bitcast_subtract_fusion
  77.5 1.0 fusion.10
  78.5 63.8 %all-reduce = (f32[64,64]{1,0:T(8,128)S(1)}, f32[]{:T(128)}) all-reduce(f32[64,64]{1,0:T(8,128)S(1)} %fusion.10, f32[]{:T(128)} %get-tuple-element.5), channel_id=1, replica_groups=mesh['parts'=2,'mem'=4,'space'=4] {'mem','space'}, use_global_device_ids=true, to_apply=%region_4.0 | all-reduce | flops 4097 | bytes 32776 | tf_op jit(solution)/shard_map/psum | solution.py:44
  142.3 0.7 broadcast_divide_fusion
  142.9 0.0 copy-start.2
  142.9 0.2 fusion.17
  143.2 0.8 fusion.18
  144.0 42.6 %all-gather.2.cloned.1.call-done = bf16[64,70,1024]{2,0,1:T(8,128)(2,1)} async-done(((bf16[16,70,1024]{2,0,1:T(8,128)(2,1)}), bf16[64,70,1024]{2,0,1:T(8,128)(2,1)}) %all-gather.2.cloned.1.call-update) | async-done | bytes 9175056 | tf_op jit(solution)/shard_map/all_gather | solution.py:25
  186.6 0.0 copy-start.1
  186.6 6.7 %convert_reduce_fusion = f32[70,1024]{1,0:T(8,128)S(1)} fusion(bf16[64,70,1024]{2,0,1:T(8,128)(2,1)} %all-gather.2.cloned.1.call-done), kind=kLoop, calls=%fused_computation | loop fusion | flops 9103360 | bytes 9461760 | tf_op jit(solution)/shard_map/reduce_sum | solution.py:29
  193.3 0.0 copy-done.2
  193.3 0.0 copy-done.1
  193.3 2.8 %add_convert_fusion = bf16[16,70,1024]{2,0,1:T(8,128)(2,1)} fusion(f32[16]{0:T(128)S(1)} %broadcast_subtract_fusion, f32[70,1024]{1,0:T(8,128)S(1)} %broadcast_multiply_fusion, bf16[64,70,1024]{2,0,1:T(8,128)(2,1)S(1)} %copy-done.1, bf16[64,16]{1,0:T(8,128)(2,1)S(1)} %constant_dynamic-slice_fusion.1), kind=kOutput, calls=%fused_computation.1 | convolution fusion | flops 150241280 | bytes 11757632 | tf_op jit(solution)/shard_map/kj,kvc->jvc/dot_general | solution.py:26
  (4 shorter events, 0.1 us)
Async XLA Ops:
  7.2 21.4 %copy-start = (bf16[64,64]{1,0:T(8,128)(2,1)S(1)}, bf16[64,64]{1,0:T(8,128)(2,1)}, u32[]{:S(2)}) copy-start(bf16[64,64]{1,0:T(8,128)(2,1)} %param.5) | copy-start | bytes 24580
  7.2 179.4 %all-gather.2.cloned.1.call-start = ((), (), s32[]{:S(2)}) async-start(), calls=%async_computation.1 | async-start | bytes 11468800 | tf_op jit(solution)/shard_map/all_gather | solution.py:25
  22.2 33.9 %all-to-all-start = ((bf16[4,2,32768]{2,1,0:T(2,128)(2,1)}), bf16[4,2,32768]{2,1,0:T(2,128)(2,1)S(1)}, u32[]{:S(2)}, u32[]{:S(2)}) async-start(bf16[4,2,32768]{2,1,0:T(2,128)(2,1)} %reshape.27), calls=%async_computation | async-start | bytes 1048576 | tf_op jit(solution)/shard_map/all_to_all | solution.py:36
  142.9 50.3 %copy-start.2 = (f32[64,64]{1,0:T(8,128)}, f32[64,64]{1,0:T(8,128)S(1)}, u32[]{:S(2)}) copy-start(f32[64,64]{1,0:T(8,128)S(1)} %broadcast_divide_fusion) | copy-start | bytes 49156
  186.6 6.7 %copy-start.1 = (bf16[64,70,1024]{2,0,1:T(8,128)(2,1)S(1)}, bf16[64,70,1024]{2,0,1:T(8,128)(2,1)}, u32[]{:S(2)}) copy-start(bf16[64,70,1024]{2,0,1:T(8,128)(2,1)} %all-gather.2.cloned.1.call-done) | copy-start | bytes 27525124
Sparse Core Ops, SparseCore 0:
  9.6 176.9 all-gather.1
where the time goes:
time: 203 us
  waiting for transfers between devices  69.2 us (34%)
  blocking collectives  63.8 us (31%)
  local copies, waits for them, and re-layouts  22.2 us (11%)
  other arithmetic  19.3 us (10%)
  between operations  14.1 us (7%)
  matrix products  7.83 us (4%)
  starting transfers between devices  6.41 us (3%)
    psum x1, blocking collectives, per_device(): lax.psum((partial_gram, weight_sum), ('mem', 'space'))  63.8 us
    all_gather x1, waiting for transfers between devices, per_device(): members_block = lax.all_gather(ensemble, 'mem', axis=0, tiled=True)  42.6 us
    all_to_all x1, waiting for transfers between devices, per_device(): lax.all_to_all(observed.astype(jnp.bfloat16), 'mem', split_axis=2, concat...  25.9 us
    unnamed x9, local copies, waits for them, and re-layouts  10.8 us
    reduce_sum x1, other arithmetic, per_device(): totals = jnp.sum(members_block, axis=0, dtype=jnp.float32)  6.65 us
    convert_element_type x1, local copies, waits for them, and re-layouts, per_device(): by_columns = lax.all_to_all(observed.astype(jnp.bfloat16), 'mem', split_a...  6.59 us
    all_to_all x1, starting transfers between devices, per_device(): lax.all_to_all(observed.astype(jnp.bfloat16), 'mem', split_axis=2, concat...  6.38 us
    convert_element_type x1, other arithmetic, per_device(): by_columns = lax.all_to_all(observed.astype(jnp.bfloat16), 'mem', split_a...  6.11 us
  transfers between devices with their start and end apart: 2, of which 2 were waited for; matrix products, arithmetic and copies ran while one was open for 20% of the time, Pallas kernels for 0%

commit v1 on v0

v1 whole, which is shorter than its diff:
```python
import functools

import jax
import jax.numpy as jnp
from jax import lax
from jax.experimental import pallas as pl
from jax.experimental.pallas import tpu as pltpu
from jax.sharding import PartitionSpec as P

HIGHEST = lax.Precision.HIGHEST
MESH = pl.DeviceIdType.MESH
LANES = 128
PIECE = 14
ROWS = 16
NT = (((1,), (1,)), ((), ()))


def dot(a, b):
    return jnp.dot(a, b, preferred_element_type=jnp.float32)


def selector(shape, match):
    rows = lax.broadcasted_iota(jnp.int32, shape, 0)
    cols = lax.broadcasted_iota(jnp.int32, shape, 1)
    return match(rows, cols)


def as_bf16(mask):
    return jnp.where(mask, 1.0, 0.0).astype(jnp.bfloat16)


def peers_of(me, size):
    if size % 2:
        return [lax.rem(me + step, size) for step in range(1, size)]
    half = size // 2
    side, place = me // half, lax.rem(me, half)
    across = [(1 - side) * half + lax.rem(place + step, half) for step in range(half)]
    return across + [side * half + lax.rem(place + step, half) for step in range(1, half)]


def when(needed, condition, body):
    if needed:
        pl.when(condition)(body)
    else:
        body()


def kernel(
    sizes, ensemble, transform, obs_operator, obs_weight, analysis, prior, posterior,
    arrived, results, observer, observed, gram, by_space, by_mem, in_slabs, out_slabs,
    in_send, in_recv, out_send, out_recv, own_in, own_out,
    space_send, space_recv, mem_send, mem_recv,
):
    n_mem, n_space, active, pieces, local, members, variables, n_obs, chunk = sizes
    blocks = members // ROWS
    aligned = local % ROWS == 0
    partial_owners = active < n_mem
    me = lax.axis_index("mem")
    here = lax.axis_index("space")
    mem_peers = peers_of(me, n_mem)
    space_peers = peers_of(here, n_space)

    def lanes_of(owner):
        return pl.ds(pl.multiple_of(owner * chunk, chunk), chunk)

    def rows_of(device):
        return pl.ds(pl.multiple_of(device * local, local), local)

    barrier = pltpu.get_barrier_semaphore()
    for peer in mem_peers:
        pl.semaphore_signal(barrier, inc=1, device_id={"mem": peer}, device_id_type=MESH)
    for peer in space_peers:
        pl.semaphore_signal(barrier, inc=1, device_id={"space": peer}, device_id_type=MESH)
    pl.semaphore_wait(barrier, n_mem - 1 + n_space - 1)

    def spot(whole, slabs, piece, device):
        start, count = pieces[piece]
        if aligned:
            return whole.at[start : start + count, rows_of(device), :]
        return slabs.at[device, start : start + count]

    def outside(array, piece, owner):
        start, count = pieces[piece]
        return array.at[start : start + count, :, lanes_of(owner)]

    def inward(piece, peer, source):
        return pltpu.make_async_remote_copy(
            src_ref=outside(ensemble, piece, peer),
            dst_ref=spot(arrived, in_slabs, piece, source),
            send_sem=in_send.at[piece, peer],
            recv_sem=in_recv.at[piece, source],
            device_id={"mem": peer},
            device_id_type=MESH,
        )

    def inward_own(piece):
        return pltpu.make_async_copy(
            outside(ensemble, piece, me), spot(arrived, in_slabs, piece, me), own_in.at[piece]
        )

    def outward(piece, peer, owner):
        return pltpu.make_async_remote_copy(
            src_ref=spot(results, out_slabs, piece, peer),
            dst_ref=outside(analysis, piece, owner),
            send_sem=out_send.at[piece, peer],
            recv_sem=out_recv.at[piece, owner],
            device_id={"mem": peer},
            device_id_type=MESH,
        )

    def outward_own(piece):
        return pltpu.make_async_copy(
            spot(results, out_slabs, piece, me), outside(analysis, piece, me), own_out.at[piece]
        )

    owns = me < active
    for piece in range(len(pieces)):
        for peer in mem_peers:
            when(partial_owners, peer < active, lambda: inward(piece, peer, me).start())
        when(partial_owners, owns, lambda: inward_own(piece).start())

    eye = as_bf16(selector((members, members), lambda r, c: r == c))
    mixing_t = lax.dot_general(eye, transform[...], NT, preferred_element_type=jnp.float32)
    keep = 1.0 - jnp.sum(mixing_t, axis=1, keepdims=True)
    ones = jnp.ones((ROWS, members), jnp.float32)
    mixer = jnp.concatenate([mixing_t, ones], axis=0).astype(jnp.bfloat16)

    obs_rows = n_obs * ROWS
    obs_pick = as_bf16(selector((obs_rows, n_obs), lambda r, c: r // ROWS == c))
    for piece, (start, count) in enumerate(pieces):
        depth = count * ROWS
        place = as_bf16(selector((variables, depth), lambda r, c: r == c // ROWS + start))
        part = dot(obs_operator[...], place).astype(jnp.bfloat16)
        mask = selector((obs_rows, depth), lambda r, c: lax.rem(r, ROWS) == lax.rem(c, ROWS))
        full = jnp.where(mask, dot(obs_pick, part), 0.0)
        observer[piece, :, 0:depth] = full.astype(jnp.bfloat16)

    def mix(piece):
        start, count = pieces[piece]
        for variable in range(start, start + count):
            if not aligned:
                for device in range(n_mem):
                    rows = slice(device * local, (device + 1) * local)
                    arrived[variable, rows, :] = in_slabs[device, variable]
            mixed = dot(mixer, arrived[variable])
            mean = mixed[members : members + 1, :] / members
            value = (mixed[:members, :] + keep * mean).astype(jnp.bfloat16)
            if aligned:
                results[variable] = value
            else:
                for device in range(n_mem):
                    rows = slice(device * local, (device + 1) * local)
                    out_slabs[device, variable] = value[rows, :]

    def observe(piece):
        start, count = pieces[piece]
        depth = count * ROWS
        for block in range(blocks):
            at = slice(block * ROWS, (block + 1) * ROWS)
            states = arrived[start : start + count, at, :].reshape(depth, chunk)
            term = dot(observer[piece, :, 0:depth], states).reshape(n_obs, ROWS, chunk)
            if piece == 0:
                observed[:, at, :] = term
            else:
                observed[:, at, :] += term

    def form_gram():
        weights = obs_weight[:, lanes_of(me)]
        total = jnp.zeros((members, members), jnp.float32)
        for quantity in range(n_obs):
            values = observed[quantity]
            departures = values - jnp.sum(values, axis=0, keepdims=True) / members
            total += lax.dot_general(
                departures * weights[quantity : quantity + 1, :],
                departures,
                NT,
                precision=HIGHEST,
                preferred_element_type=jnp.float32,
            )
        gram[0:members, 0:members] = total
        gram[members : members + 8, :] = jnp.full((8, LANES), jnp.sum(weights), jnp.float32)

    gram[...] = jnp.zeros_like(gram)

    def work():
        for piece in range(len(pieces)):
            for peer in mem_peers:
                inward(piece, me, peer).wait_recv()
            inward_own(piece).wait()
            mix(piece)
            for peer in mem_peers:
                outward(piece, peer, me).start()
            outward_own(piece).start()
            observe(piece)
        form_gram()

    when(partial_owners, owns, work)

    def exchange(source, slots, index, peers, axis, send, recv):
        slots[index] = source
        copies = [
            pltpu.make_async_remote_copy(
                src_ref=slots.at[index],
                dst_ref=slots.at[index],
                send_sem=send.at[peer],
                recv_sem=recv.at[index],
                device_id={axis: peer},
                device_id_type=MESH,
            )
            for peer in peers
        ]
        for copy in copies:
            copy.start()
        for peer in peers:
            pltpu.make_async_remote_copy(
                src_ref=slots.at[peer],
                dst_ref=slots.at[peer],
                send_sem=send.at[peer],
                recv_sem=recv.at[peer],
                device_id={axis: peer},
                device_id_type=MESH,
            ).wait_recv()
        total = slots[0]
        for slot in range(1, slots.shape[0]):
            total += slots[slot]
        for copy in copies:
            copy.wait_send()
        return total

    total = exchange(gram[...], by_space, here, space_peers, "space", space_send, space_recv)
    total = exchange(total, by_mem, me, mem_peers, "mem", mem_send, mem_recv)
    prior_gram = total[0:members, 0:members] / total[members : members + 1, 0:members]
    prior[...] = prior_gram
    carried = jnp.dot(
        mixing_t, prior_gram, precision=HIGHEST, preferred_element_type=jnp.float32
    )
    posterior[...] = jnp.dot(
        carried,
        transform[...].astype(jnp.float32),
        precision=HIGHEST,
        preferred_element_type=jnp.float32,
    )

    for piece in range(len(pieces)):
        for peer in mem_peers:
            when(partial_owners, peer < active, lambda: inward(piece, peer, me).wait_send())
            when(partial_owners, owns, lambda: outward(piece, peer, me).wait_send())
            when(partial_owners, peer < active, lambda: outward(piece, me, peer).wait_recv())
        when(partial_owners, owns, lambda: outward_own(piece).wait())


def per_device(n_mem, n_space, ensemble, transform, obs_operator, obs_weight):
    local, variables, cells = ensemble.shape
    members = transform.shape[0]
    n_obs = obs_operator.shape[0]
    active = min(n_mem, cells // LANES)
    chunk = cells // active
    pieces = tuple(
        (start, min(PIECE, variables - start)) for start in range(0, variables, PIECE)
    )
    sizes = (n_mem, n_space, active, pieces, local, members, variables, n_obs, chunk)
    vmem = pl.BlockSpec(memory_space=pltpu.VMEM)
    any_space = pl.BlockSpec(memory_space=pl.ANY)
    gram_shape = (members + 8, LANES)
    slabs = (1, 1, ROWS, LANES) if local % ROWS == 0 else (n_mem, variables, local, chunk)
    dma = pltpu.SemaphoreType.DMA
    by_variable, prior, posterior = pl.pallas_call(
        functools.partial(kernel, sizes),
        out_shape=(
            jax.ShapeDtypeStruct((variables, local, cells), jnp.bfloat16),
            jax.ShapeDtypeStruct((members, members), jnp.float32),
            jax.ShapeDtypeStruct((members, members), jnp.float32),
        ),
        in_specs=[any_space, vmem, vmem, vmem],
        out_specs=(any_space, vmem, vmem),
        scratch_shapes=[
            pltpu.VMEM((variables, members, chunk), jnp.bfloat16),
            pltpu.VMEM((variables, members, chunk), jnp.bfloat16),
            pltpu.VMEM((len(pieces), n_obs * ROWS, PIECE * ROWS), jnp.bfloat16),
            pltpu.VMEM((n_obs, members, chunk), jnp.float32),
            pltpu.VMEM(gram_shape, jnp.float32),
            pltpu.VMEM((n_space,) + gram_shape, jnp.float32),
            pltpu.VMEM((n_mem,) + gram_shape, jnp.float32),
            pltpu.VMEM(slabs, jnp.bfloat16),
            pltpu.VMEM(slabs, jnp.bfloat16),
            dma((len(pieces), n_mem)),
            dma((len(pieces), n_mem)),
            dma((len(pieces), n_mem)),
            dma((len(pieces), n_mem)),
            dma((len(pieces),)),
            dma((len(pieces),)),
            dma((n_space,)),
            dma((n_space,)),
            dma((n_mem,)),
            dma((n_mem,)),
        ],
        compiler_params=pltpu.CompilerParams(collective_id=0, has_side_effects=True),
        name="ensemble_exchange",
    )(jnp.transpose(ensemble, (1, 0, 2)), transform, obs_operator, obs_weight)
    return jnp.transpose(by_variable, (1, 0, 2)), prior, posterior


def solution(mesh):
    return jax.shard_map(
        functools.partial(per_device, mesh.shape["mem"], mesh.shape["space"]),
        mesh=mesh,
        in_specs=(
            P("mem", None, ("parts", "space")),
            P("parts", None),
            P(),
            P(None, ("parts", "space")),
        ),
        out_specs=(P("mem", None, ("parts", "space")), P("parts", None), P("parts", None)),
        check_vma=False,
    )
```

time: 203 us -> 117 us (0.58)
  Pallas kernels: 0 us -> 111 us
  waiting for transfers between devices: 69.2 us -> 0 us
  blocking collectives: 63.8 us -> 0 us
  other arithmetic: 19.3 us -> 0 us
  local copies, waits for them, and re-layouts: 22.2 us -> 4.63 us
  between operations: 14.1 us -> 0.66 us
  matrix products: 7.83 us -> 0 us
  starting transfers between devices: 6.41 us -> 0 us
    pallas_call x0 -> x1, Pallas kernels: none -> 111 us  [per_device(): pl.pallas_call(functools.partial(kernel, sizes), out_shape=(jax.ShapeDtyp...]
    psum x1 -> x0, blocking collectives: 63.8 us -> none  [per_device(): lax.psum((partial_gram, weight_sum), ('mem', 'space'))]
    all_gather x1 -> x0, waiting for transfers between devices: 42.6 us -> none  [per_device(): members_block = lax.all_gather(ensemble, 'mem', axis=0, tiled=True)]
    all_to_all x1 -> x0, waiting for transfers between devices: 25.9 us -> none  [per_device(): lax.all_to_all(observed.astype(jnp.bfloat16), 'mem', split_axis=2, concat...]
    reduce_sum x5 -> x0, other arithmetic: 12.4 us -> none  [the longest x1 6.65 us: per_device(): totals = jnp.sum(members_block, axis=0, dtype=jnp.float32)]
    convert_element_type x2 -> x0, local copies, waits for them, and re-layouts: 11.3 us -> none  [the longest x1 6.59 us: per_device(): by_columns = lax.all_to_all(observed.astype(jnp.bfloat16), 'mem', split_a...]
    dot_general x5 -> x0, matrix products: 7.83 us -> none  [the longest x1 2.98 us: per_device(): jnp.einsum('ov,mvc->moc', obs_operator, ensemble, preferred_element_type=...]
    all_to_all x1 -> x0, starting transfers between devices: 6.38 us -> none  [per_device(): lax.all_to_all(observed.astype(jnp.bfloat16), 'mem', split_axis=2, concat...]
  transfers between devices with their start and end apart: 2 -> 0, of which waited for: 2 -> 0; matrix products, arithmetic and copies ran while one was open for 20% -> 0% of each run, Pallas kernels for 0% -> 0%
where the time goes in v1:
time: 117 us; the launch traced here: 116 us
  Pallas kernels  111 us (95%)
  local copies, waits for them, and re-layouts  4.63 us (4%)
    pallas_call x1, Pallas kernels, per_device(): pl.pallas_call(functools.partial(kernel, sizes), out_shape=(jax.ShapeDtyp...  111 us
    unnamed x7, local copies, waits for them, and re-layouts  4.63 us

profile of v1, /device:TPU:0, one launch (start us, length us, event | category | flops | bytes accessed | tf_op | source)
XLA Modules:
  0.0 116.3 jit_solution(4973941495048075479)
XLA Ops:
  0.6 111.0 %ensemble_exchange.1 = (bf16[70,16,1024]{2,1,0:T(8,128)(2,1)}, f32[64,64]{1,0:T(8,128)}, f32[64,64]{1,0:T(8,128)}) custom-call(bf16[70,16,1024]{2,1,0:T(8,128)(2,1)} %bitcast.2, bf16[64,64]{1,0:T(8,128)(2,1)} %transform.1, bf16[16,70]{1,0:T(8,128)(2,1)} %obs_operator.1, f32[16,1024]{1,0:T(8,128)} %obs_weight.1), custom_call_target="tpu_custom_call" | custom-call | tf_op jit(solution)/shard_map/ensemble_exchange/pallas_call | solution.py:267
  111.7 0.0 copy-start.1
  111.7 0.0 copy-start
  111.7 3.4 %copy.10 = bf16[16,70,1024]{2,0,1:T(8,128)(2,1)} copy(bf16[16,70,1024]{2,0,1:T(8,128)(2,1)} %bitcast.3) | data formatting | bytes 4587520
  115.1 0.0 copy-done.1
  115.1 0.6 copy.11
  115.7 0.0 copy-done
  115.7 0.6 copy.12
Async XLA Ops:
  111.7 3.4 %copy-start.1 = (f32[64,64]{1,0:T(8,128)S(1)}, f32[64,64]{1,0:T(8,128)}, u32[]{:S(2)}) copy-start(f32[64,64]{1,0:T(8,128)} %get-tuple-element.13) | copy-start | bytes 49156
  111.7 4.0 %copy-start = (f32[64,64]{1,0:T(8,128)S(1)}, f32[64,64]{1,0:T(8,128)}, u32[]{:S(2)}) copy-start(f32[64,64]{1,0:T(8,128)} %get-tuple-element.14) | copy-start | bytes 49156

commit v2 on v1

--- a/solution.py
+++ b/solution.py
@@ -31,11 +31,11 @@
 
 def peers_of(me, size):
     if size % 2:
-        return [lax.rem(me + step, size) for step in range(1, size)]
+        return [lax.rem(me + step, size) for step in range(1, size)], []
     half = size // 2
     side, place = me // half, lax.rem(me, half)
     across = [(1 - side) * half + lax.rem(place + step, half) for step in range(half)]
-    return across + [side * half + lax.rem(place + step, half) for step in range(1, half)]
+    return across, [side * half + lax.rem(place + step, half) for step in range(1, half)]
 
 
 def when(needed, condition, body):
@@ -46,19 +46,25 @@
 
 
 def kernel(
-    sizes, ensemble, transform, obs_operator, obs_weight, analysis, prior, posterior,
+    sizes, ensemble, *refs,
+):
+    smalls, refs = refs[:3], refs[3:]
+    analysis, prior, posterior, transform, obs_operator, obs_weight, small_sem = refs[:7]
+    (
     arrived, results, observer, observed, gram, by_space, by_mem, in_slabs, out_slabs,
     in_send, in_recv, out_send, out_recv, own_in, own_out,
     space_send, space_recv, mem_send, mem_recv,
-):
+    ) = refs[7:]
     n_mem, n_space, active, pieces, local, members, variables, n_obs, chunk = sizes
     blocks = members // ROWS
     aligned = local % ROWS == 0
     partial_owners = active < n_mem
     me = lax.axis_index("mem")
     here = lax.axis_index("space")
-    mem_peers = peers_of(me, n_mem)
-    space_peers = peers_of(here, n_space)
+    across, beside = peers_of(me, n_mem)
+    mem_peers = across + beside
+    space_peers = sum(peers_of(here, n_space), [])
+    central = jnp.logical_or(me * 2 == n_mem, (me + 1) * 2 == n_mem)
 
     def lanes_of(owner):
         return pl.ds(pl.multiple_of(owner * chunk, chunk), chunk)
@@ -114,10 +120,22 @@
         )
 
     owns = me < active
+    for group in (beside, across):
+        for piece in range(len(pieces)):
+            for peer in group:
+                when(partial_owners, peer < active, lambda: inward(piece, peer, me).start())
     for piece in range(len(pieces)):
-        for peer in mem_peers:
-            when(partial_owners, peer < active, lambda: inward(piece, peer, me).start())
         when(partial_owners, owns, lambda: inward_own(piece).start())
+    loads = [
+        pltpu.make_async_copy(source, target, small_sem.at[index])
+        for index, (source, target) in enumerate(
+            zip(smalls, (transform, obs_operator, obs_weight))
+        )
+    ]
+    for load in loads:
+        load.start()
+    for load in loads:
+        load.wait()
 
     eye = as_bf16(selector((members, members), lambda r, c: r == c))
     mixing_t = lax.dot_general(eye, transform[...], NT, preferred_element_type=jnp.float32)
@@ -182,21 +200,33 @@
 
     gram[...] = jnp.zeros_like(gram)
 
+    last = len(pieces) - 1
+
+    def send_back(piece, group):
+        for peer in group:
+            outward(piece, peer, me).start()
+
     def work():
-        for piece in range(len(pieces)):
+        for piece in range(last + 1):
             for peer in mem_peers:
                 inward(piece, me, peer).wait_recv()
             inward_own(piece).wait()
             mix(piece)
-            for peer in mem_peers:
-                outward(piece, peer, me).start()
+            send_back(piece, beside)
+            if piece < last:
+                pl.when(central)(lambda: send_back(piece, across))
             outward_own(piece).start()
             observe(piece)
         form_gram()
 
+    def finish_sends():
+        for piece in range(last):
+            pl.when(jnp.logical_not(central))(lambda: send_back(piece, across))
+        send_back(last, across)
+
     when(partial_owners, owns, work)
 
-    def exchange(source, slots, index, peers, axis, send, recv):
+    def exchange(source, slots, index, peers, axis, send, recv, between):
         slots[index] = source
         copies = [
             pltpu.make_async_remote_copy(
@@ -211,6 +241,7 @@
         ]
         for copy in copies:
             copy.start()
+        between()
         for peer in peers:
             pltpu.make_async_remote_copy(
                 src_ref=slots.at[peer],
@@ -227,8 +258,13 @@
             copy.wait_send()
         return total
 
-    total = exchange(gram[...], by_space, here, space_peers, "space", space_send, space_recv)
-    total = exchange(total, by_mem, me, mem_peers, "mem", mem_send, mem_recv)
+    total = exchange(
+        gram[...], by_space, here, space_peers, "space", space_send, space_recv, lambda: None
+    )
+    total = exchange(
+        total, by_mem, me, mem_peers, "mem", mem_send, mem_recv,
+        lambda: when(partial_owners, owns, finish_sends),
+    )
     prior_gram = total[0:members, 0:members] / total[members : members + 1, 0:members]
     prior[...] = prior_gram
     carried = jnp.dot(
@@ -267,13 +303,17 @@
     by_variable, prior, posterior = pl.pallas_call(
         functools.partial(kernel, sizes),
         out_shape=(
-            jax.ShapeDtypeStruct((variables, local, cells), jnp.bfloat16),
-            jax.ShapeDtypeStruct((members, members), jnp.float32),
-            jax.ShapeDtypeStruct((members, members), jnp.float32),
+            pltpu.VMEM((variables, local, cells), jnp.bfloat16),
+            pltpu.VMEM((members, members), jnp.float32),
+            pltpu.VMEM((members, members), jnp.float32),
         ),
-        in_specs=[any_space, vmem, vmem, vmem],
-        out_specs=(any_space, vmem, vmem),
+        in_specs=[any_space] * 4,
+        out_specs=(vmem, vmem, vmem),
         scratch_shapes=[
+            pltpu.VMEM(transform.shape, jnp.bfloat16),
+            pltpu.VMEM(obs_operator.shape, jnp.bfloat16),
+            pltpu.VMEM(obs_weight.shape, jnp.float32),
+            dma((3,)),
             pltpu.VMEM((variables, members, chunk), jnp.bfloat16),
             pltpu.VMEM((variables, members, chunk), jnp.bfloat16),
             pltpu.VMEM((len(pieces), n_obs * ROWS, PIECE * ROWS), jnp.bfloat16),

time: 117 us -> 111 us (0.949)
  Pallas kernels: 111 us -> 108 us
  local copies, waits for them, and re-layouts: 4.63 us -> 2.61 us
    pallas_call x1, Pallas kernels: 111 us -> 108 us  [per_device(): pl.pallas_call(functools.partial(kernel, sizes), out_shape=(pltpu.VMEM((v...]
    unnamed x7 -> x3, local copies, waits for them, and re-layouts: 4.63 us -> 2.61 us
where the time goes in v2:
time: 111 us
  Pallas kernels  108 us (97%)
  local copies, waits for them, and re-layouts  2.61 us (2%)
    pallas_call x1, Pallas kernels, per_device(): pl.pallas_call(functools.partial(kernel, sizes), out_shape=(pltpu.VMEM((v...  108 us
    unnamed x3, local copies, waits for them, and re-layouts  2.61 us

profile of v2, /device:TPU:0, one launch (start us, length us, event | category | flops | bytes accessed | tf_op | source)
XLA Modules:
  0.0 110.9 jit_solution(12549933806288911813)
XLA Ops:
  0.6 107.6 %ensemble_exchange.1 = (bf16[70,16,1024]{2,1,0:T(8,128)(2,1)S(1)}, f32[64,64]{1,0:T(8,128)S(1)}, f32[64,64]{1,0:T(8,128)S(1)}) custom-call(bf16[70,16,1024]{2,1,0:T(8,128)(2,1)} %bitcast.3, bf16[64,64]{1,0:T(8,128)(2,1)} %refs_0_.1, bf16[16,70]{1,0:T(8,128)(2,1)} %refs_1_.1, f32[16,1024]{1,0:T(8,128)} %refs_2_.1), custom_call_target="tpu_custom_call" | custom-call | tf_op jit(solution)/shard_map/ensemble_exchange/pallas_call | solution.py:303
  108.2 1.4 %copy.10 = bf16[16,70,1024]{2,0,1:T(8,128)(2,1)} copy(bf16[16,70,1024]{2,0,1:T(8,128)(2,1)S(1)} %bitcast.2) | data formatting | bytes 4587520
  109.6 0.6 copy.11
  110.2 0.6 copy.12

commit v3 on v2

--- a/solution.py
+++ b/solution.py
@@ -283,6 +283,39 @@
             when(partial_owners, owns, lambda: outward(piece, peer, me).wait_send())
             when(partial_owners, peer < active, lambda: outward(piece, me, peer).wait_recv())
         when(partial_owners, owns, lambda: outward_own(piece).wait())
+
+
+def store(*refs):
+    count = len(refs) // 2
+    sources, targets, sems = refs[:count], refs[count : 2 * count], refs[-1]
+    pairs = []
+    for source, target in zip(sources, targets):
+        if len(source.shape) == 3:
+            for start in range(0, source.shape[0], PIECE):
+                part = slice(start, min(start + PIECE, source.shape[0]))
+                pairs.append((source.at[part], target.at[part]))
+        else:
+            pairs.append((source, target))
+    copies = [
+        pltpu.make_async_copy(source, target, sems.at[index])
+        for index, (source, target) in enumerate(pairs)
+    ]
+    for copy in copies:
+        copy.start()
+    for copy in copies:
+        copy.wait()
+
+
+def write_out(*arrays):
+    return pl.pallas_call(
+        store,
+        out_shape=tuple(jax.ShapeDtypeStruct(a.shape, a.dtype) for a in arrays),
+        in_specs=[pl.BlockSpec(memory_space=pl.ANY)] * len(arrays),
+        out_specs=tuple([pl.BlockSpec(memory_space=pl.ANY)] * len(arrays)),
+        scratch_shapes=[pltpu.SemaphoreType.DMA((len(arrays) + pl.cdiv(arrays[0].shape[0], PIECE),))],
+        compiler_params=pltpu.CompilerParams(vmem_limit_bytes=8 << 20),
+        name="store_outputs",
+    )(*arrays)
 
 
 def per_device(n_mem, n_space, ensemble, transform, obs_operator, obs_weight):
@@ -337,6 +370,7 @@
         compiler_params=pltpu.CompilerParams(collective_id=0, has_side_effects=True),
         name="ensemble_exchange",
     )(jnp.transpose(ensemble, (1, 0, 2)), transform, obs_operator, obs_weight)
+    by_variable, prior, posterior = write_out(by_variable, prior, posterior)
     return jnp.transpose(by_variable, (1, 0, 2)), prior, posterior
 
 

time: 111 us -> 110 us (level)
  local copies, waits for them, and re-layouts: 2.61 us -> 0 us
    unnamed x3 -> x0, local copies, waits for them, and re-layouts: 2.61 us -> none
    pallas_call x0 -> x1, Pallas kernels: none -> 1.45 us  [write_out(): pl.pallas_call(store, out_shape=tuple((jax.ShapeDtypeStruct(a.shape, a.dt...]
where the time goes in v3:
time: 110 us
  Pallas kernels  109 us (99%)
    pallas_call x1, Pallas kernels, per_device(): pl.pallas_call(functools.partial(kernel, sizes), out_shape=(pltpu.VMEM((v...  108 us

profile of v3, /device:TPU:0, one launch (start us, length us, event | category | flops | bytes accessed | tf_op | source)
XLA Modules:
  0.0 109.7 jit_solution(10464401679022857413)
XLA Ops:
  0.6 107.6 %ensemble_exchange.1 = (bf16[70,16,1024]{2,1,0:T(8,128)(2,1)S(1)}, f32[64,64]{1,0:T(8,128)S(1)}, f32[64,64]{1,0:T(8,128)S(1)}) custom-call(bf16[70,16,1024]{2,1,0:T(8,128)(2,1)} %bitcast.2, bf16[64,64]{1,0:T(8,128)(2,1)} %refs_0_.1, bf16[16,70]{1,0:T(8,128)(2,1)} %refs_1_.1, f32[16,1024]{1,0:T(8,128)} %refs_2_.1), custom_call_target="tpu_custom_call" | custom-call | tf_op jit(solution)/shard_map/ensemble_exchange/pallas_call | solution.py:336
  108.2 1.5 %store_outputs.1 = (bf16[70,16,1024]{2,1,0:T(8,128)(2,1)}, f32[64,64]{1,0:T(8,128)}, f32[64,64]{1,0:T(8,128)}) custom-call(bf16[70,16,1024]{2,1,0:T(8,128)(2,1)S(1)} %get-tuple-element.9.refs_0_, f32[64,64]{1,0:T(8,128)S(1)} %get-tuple-element.10.refs_1_, f32[64,64]{1,0:T(8,128)S(1)} %get-tuple-element.11.refs_2_), custom_call_target="tpu_custom_call" | custom-call | tf_op jit(solution)/shard_map/store_outputs/pallas_call | solution.py:310
